TPU v7x, 32 devices: a whole 2x2x4 slice. The times are simulated.
32 devices in a mesh: pp: 8 (over z, y), ep: 4 (over x, core).
Axes of the slice: x: 2, y: 2, z: 4, core: 2. Of those that a mesh axis runs over, the one named last changes fastest.
Arguments:
- expert_out: bfloat16 [8, 64, 160, 3584], P('pp', 'ep')
- expert_ids: int32 [8, 4, 256, 8], P('pp', 'ep')
- slot_ids: int32 [8, 4, 256, 8], P('pp', 'ep')
- gate_vals: float32 [8, 4, 256, 8], P('pp', 'ep')
- residual: bfloat16 [8, 4, 256, 3584], P('pp', 'ep')
- norm_w: float32 [8, 3584], P('pp')
- w_query: bfloat16 [8, 3584, 28, 128], P('pp')
- w_key: bfloat16 [8, 3584, 28, 128], P('pp')
- w_value: bfloat16 [8, 3584, 28, 128], P('pp')
- w_out: bfloat16 [8, 28, 128, 3584], P('pp')
Outputs:
- output: bfloat16 [8, 4, 256, 3584], P('pp', 'ep')
All inputs are finite; a program needn't handle non-finite values.
Results may differ from a plain program's by a relative error of at most 0.0131893.
Values are sent between devices in bfloat16 or wider.
A program may use at most 1 GiB of HBM per device.

v0:
```python
import jax
import jax.numpy as jnp
from jax import lax
from jax.sharding import PartitionSpec as P

NORM_EPS = 1e-6


def gated_sum(exp_table, expert_ids, slot_pos, gate_vals, residual):
    is_kept = slot_pos >= 0
    pick_rows = jax.vmap(lambda exp_rows, id_blk, pos_blk: exp_rows[id_blk, pos_blk])
    picked = pick_rows(exp_table, expert_ids, jnp.where(is_kept, slot_pos, 0))
    weight = jnp.where(is_kept, gate_vals, 0.0)
    mixed_sum = residual.astype(jnp.float32) + jnp.sum(weight[..., None] * picked.astype(jnp.float32), axis=3)
    return mixed_sum.astype(jnp.bfloat16)


def attention_block(combined, norm_w, w_query, w_key, w_value, w_out):
    y_wide = combined.astype(jnp.float32)
    inv_rms = lax.rsqrt(jnp.mean(y_wide * y_wide, axis=-1, keepdims=True) + NORM_EPS)
    x_in = (y_wide * inv_rms * norm_w).astype(jnp.bfloat16)
    q_heads = jnp.einsum('bld,dhe->blhe', x_in, w_query, preferred_element_type=jnp.float32).astype(jnp.bfloat16)
    k_heads = jnp.einsum('bld,dhe->blhe', x_in, w_key, preferred_element_type=jnp.float32).astype(jnp.bfloat16)
    v_heads = jnp.einsum('bld,dhe->blhe', x_in, w_value, preferred_element_type=jnp.float32).astype(jnp.bfloat16)
    head_dim = w_query.shape[2]
    seq_len = combined.shape[1]
    scores = jnp.einsum('bqhe,bkhe->bhqk', q_heads, k_heads, preferred_element_type=jnp.float32) * (head_dim ** -0.5)
    causal = jnp.arange(seq_len)[:, None] >= jnp.arange(seq_len)[None, :]
    attn_probs = jax.nn.softmax(jnp.where(causal, scores, -jnp.inf), axis=-1).astype(jnp.bfloat16)
    attn_out = jnp.einsum('bhqk,bkhe->bqhe', attn_probs, v_heads, preferred_element_type=jnp.float32).astype(jnp.bfloat16)
    out_proj = jnp.einsum('crif,ife->cre', attn_out, w_out, preferred_element_type=jnp.float32).astype(jnp.bfloat16)
    return (y_wide + out_proj.astype(jnp.float32)).astype(jnp.bfloat16)


def solution(mesh):
    stages = mesh.shape['pp']
    group_size = mesh.shape['ep']
    send_next = [(src_row, (src_row + 1) % stages) for src_row in range(stages)]
    tok_spec = P('pp', 'ep', None, None)
    wt_spec = P('pp', None, None, None)

    def device_step(expert_out, expert_ids, slot_ids, gate_vals, residual, norm_w, w_query, w_key, w_value, w_out):
        num_micro, seqs_dev, seq_len, d_model = residual.shape
        src_slots = expert_out.shape[2] // group_size
        returned = lax.all_to_all(expert_out, 'ep', 2, 1, tiled=True)
        block_base = lax.axis_index('ep') * src_slots
        slot_pos = jnp.where(slot_ids >= 0, slot_ids - block_base, -1)
        combined = gated_sum(returned, expert_ids, slot_pos, gate_vals, residual)
        arrived = lax.ppermute(combined, 'pp', send_next)
        flat_in = arrived.reshape(num_micro * seqs_dev, seq_len, d_model)
        result = attention_block(flat_in, norm_w[0], w_query[0], w_key[0], w_value[0], w_out[0])
        return result.reshape(num_micro, seqs_dev, seq_len, d_model)

    return jax.shard_map(device_step, mesh=mesh, in_specs=(tok_spec, tok_spec, tok_spec, tok_spec, tok_spec, P('pp', None), wt_spec, wt_spec, wt_spec, wt_spec), out_specs=tok_spec, check_vma=False)
```

profile of v0, /device:TPU:0, one launch (start us, length us, event | category | flops | bytes accessed | tf_op | source)
XLA Modules:
  0.0 469.7 jit_solution(13467876054336709439)
XLA Ops:
  0.0 20.4 %copy.21 = bf16[1,16,160,3584]{3,1,0,2:T(8,128)(2,1)} copy(bf16[1,16,160,3584]{3,2,1,0:T(8,128)(2,1)} %param.10) | data formatting | bytes 36700160 | tf_op args[0]
  20.4 0.0 copy-start.1
  20.4 0.0 copy-start.4
  20.4 0.0 copy-start.3
  20.4 7.4 %all-to-all-start = ((bf16[1,16,160,3584]{3,1,0,2:T(8,128)(2,1)}), bf16[1,16,160,3584]{3,1,0,2:T(8,128)(2,1)}, u32[]{:S(2)}, u32[]{:S(2)}) async-start(bf16[1,16,160,3584]{3,1,0,2:T(8,128)(2,1)} %copy.21), calls=%async_computation | async-start | bytes 36700160 | tf_op jit(solution)/shard_map/all_to_all | solution.py:45
  27.8 0.0 copy-done.1
  27.8 0.0 copy-done.4
  27.9 0.1 copy.23
  28.0 0.1 reshape.182
  28.1 0.0 copy-done.3
  28.2 0.1 copy.20
  28.3 199.8 %all-to-all-done = bf16[1,16,160,3584]{3,1,0,2:T(8,128)(2,1)} async-done(((bf16[1,16,160,3584]{3,1,0,2:T(8,128)(2,1)}), bf16[1,16,160,3584]{3,1,0,2:T(8,128)(2,1)}, u32[]{:S(2)}, u32[]{:S(2)}) %all-to-all-start) | async-done | bytes 18350112 | tf_op jit(solution)/shard_map/all_to_all | solution.py:45
  228.1 20.5 %copy.22 = bf16[1,16,4,40,3584]{4,3,1,2,0:T(8,128)(2,1)} copy(bf16[1,16,4,40,3584]{4,1,3,2,0:T(8,128)(2,1)} %bitcast.1) | data formatting | bytes 36700160 | tf_op jit(solution)/shard_map/all_to_all | solution.py:45
  248.6 71.3 %gather_fusion = bf16[2048,3584]{1,0:T(8,128)(2,1)} fusion(bf16[1,64,40,3584]{3,2,1,0:T(8,128)(2,1)} %bitcast.82, s32[2048]{0:T(1024)S(1)} %reshape.182), kind=kCustom, calls=%fused_computation | custom fusion | bytes 29384704 | tf_op jit(solution)/shard_map/vmap()/gather | solution.py:11
  319.9 0.0 copy-start
  319.9 32.5 %fusion.1 = f32[256,3584]{1,0:T(8,128)S(1)} fusion(bf16[2048,3584]{1,0:T(8,128)(2,1)} %gather_fusion, f32[256,8]{1,0:T(8,128)S(1)} %copy.20), kind=kLoop, calls=%fused_computation.3 | loop fusion | flops 21102592 | bytes 18358272 | tf_op jit(solution)/shard_map/reduce_sum | solution.py:14
  352.4 0.0 copy-done
  352.4 0.0 copy-start.2
  352.4 0.4 fusion.25
  352.8 2.2 collective-permute-start
  355.0 0.0 copy-done.2
  355.1 44.6 %collective-permute-done = bf16[1,1,256,3584]{3,2,1,0:T(8,128)(2,1)} collective-permute-done((bf16[1,1,256,3584]{3,2,1,0:T(8,128)(2,1)S(1)}, bf16[1,1,256,3584]{3,2,1,0:T(8,128)(2,1)}, u32[]{:S(2)}, u32[]{:S(2)}) %collective-permute-start) | collective-permute-done | bytes 1835040 | tf_op jit(solution)/shard_map/ppermute | solution.py:49
  399.7 1.9 fusion.22
  401.6 12.4 %fusion.6 = bf16[256,28,128]{2,0,1:T(8,128)(2,1)S(1)} fusion(bf16[1,3584,28,128]{3,1,2,0:T(8,128)(2,1)} %param.16, bf16[1,1,256,3584]{3,2,1,0:T(8,128)(2,1)} %collective-permute-done, f32[3584]{0:T(1024)S(1)} %reduce.7, f32[256]{0:T(256)S(1)} %add_rsqrt_fusion), kind=kOutput, calls=%fused_computation.8 | convolution fusion | flops 6580338688 | bytes 29375488 | tf_op jit(solution)/shard_map/bld,dhe->blhe/dot_general | solution.py:22
  414.1 15.5 %fusion.38 = f32[28,256,256]{1,2,0:T(8,128)} fusion(bf16[1,3584,28,128]{3,1,2,0:T(8,128)(2,1)} %param.17, bf16[256,28,128]{2,0,1:T(8,128)(2,1)S(1)} %fusion.6, bf16[1,1,256,3584]{3,2,1,0:T(8,128)(2,1)} %collective-permute-done, f32[3584]{0:T(1024)S(1)} %reduce.7, f32[256]{0:T(256)S(1)} %add_rsqrt_fusion), kind=kOutput, calls=%fused_computation.37 | convolution fusion | flops 7051018240 | bytes 36715520 | tf_op jit(solution)/shard_map/bqhe,bkhe->bhqk/dot_general | solution.py:27
  429.6 10.8 %fusion.61 = (f32[28,256]{1,0:T(8,128)S(1)}, f32[28,256,256]{1,2,0:T(8,128)}) fusion(f32[28,256,256]{1,2,0:T(8,128)} %fusion.38, pred[256,256]{0,1:T(8,128)(4,1)S(1)} %iota_compare_fusion), kind=kOutput, calls=%fused_computation.63 | output fusion | flops 11010303 | bytes 14774272 | tf_op jit(solution)/shard_map/sub | solution.py:29
  440.4 12.4 %fusion.8 = bf16[256,28,128]{2,0,1:T(8,128)(2,1)S(1)} fusion(bf16[1,3584,28,128]{3,1,2,0:T(8,128)(2,1)} %param.18, bf16[1,1,256,3584]{3,2,1,0:T(8,128)(2,1)} %collective-permute-done, f32[3584]{0:T(1024)S(1)} %reduce.7, f32[256]{0:T(256)S(1)} %add_rsqrt_fusion), kind=kOutput, calls=%fused_computation.10 | convolution fusion | flops 6580338688 | bytes 29375488 | tf_op jit(solution)/shard_map/bld,dhe->blhe/dot_general | solution.py:24
  452.8 17.0 %fusion.31 = bf16[1,1,256,3584]{3,2,1,0:T(8,128)(2,1)} fusion(bf16[1,1,256,3584]{3,2,1,0:T(8,128)(2,1)} %collective-permute-done, bf16[1,28,128,3584]{3,2,1,0:T(8,128)(2,1)} %param.19, f32[28,256,256]{1,2,0:T(8,128)} %get-tuple-element.6, f32[28,256]{1,0:T(8,128)S(1)} %get-tuple-element.5, bf16[256,28,128]{2,0,1:T(8,128)(2,1)S(1)} %fusion.8), kind=kOutput, calls=%fused_computation.34 | convolution fusion | flops 7055605760 | bytes 38563840 | tf_op jit(solution)/shard_map/crif,ife->cre/dot_general | solution.py:31
  (8 shorter events, 0.1 us)
Async XLA Ops:
  20.4 7.4 %copy-start.1 = (s32[1,1,256,8]{2,3,1,0:T(8,128)S(1)}, s32[1,1,256,8]{2,3,1,0:T(8,128)}, u32[]{:S(2)}) copy-start(s32[1,1,256,8]{2,3,1,0:T(8,128)} %param.12) | copy-start | bytes 24580
  20.4 7.4 %copy-start.4 = (s32[1,1,256,8]{2,3,1,0:T(8,128)S(1)}, s32[1,1,256,8]{2,3,1,0:T(8,128)}, u32[]{:S(2)}) copy-start(s32[1,1,256,8]{2,3,1,0:T(8,128)} %param.11) | copy-start | bytes 24580
  20.4 7.7 %copy-start.3 = (f32[1,1,256,8]{2,3,1,0:T(8,128)S(1)}, f32[1,1,256,8]{2,3,1,0:T(8,128)}, u32[]{:S(2)}) copy-start(f32[1,1,256,8]{2,3,1,0:T(8,128)} %param.13) | copy-start | bytes 24580
  20.4 207.6 %all-to-all-start = ((bf16[1,16,160,3584]{3,1,0,2:T(8,128)(2,1)}), bf16[1,16,160,3584]{3,1,0,2:T(8,128)(2,1)}, u32[]{:S(2)}, u32[]{:S(2)}) async-start(bf16[1,16,160,3584]{3,1,0,2:T(8,128)(2,1)} %copy.21), calls=%async_computation | async-start | bytes 36700160 | tf_op jit(solution)/shard_map/all_to_all | solution.py:45
  319.9 32.5 %copy-start = (bf16[1,1,256,3584]{3,2,1,0:T(8,128)(2,1)S(1)}, bf16[1,1,256,3584]{3,2,1,0:T(8,128)(2,1)}, u32[]{:S(2)}) copy-start(bf16[1,1,256,3584]{3,2,1,0:T(8,128)(2,1)} %param.14) | copy-start | bytes 5505028
  352.4 2.7 copy-start.2
  352.8 46.9 %collective-permute-start = (bf16[1,1,256,3584]{3,2,1,0:T(8,128)(2,1)S(1)}, bf16[1,1,256,3584]{3,2,1,0:T(8,128)(2,1)}, u32[]{:S(2)}, u32[]{:S(2)}) collective-permute-start(bf16[1,1,256,3584]{3,2,1,0:T(8,128)(2,1)S(1)} %fusion.25), channel_id=1, source_target_pairs={{0,4},{4,8},{8,12},{12,16},{16,20},{20,24},{24,28},{28,0},{1,5},{5... | collective-permute-start | bytes 5505032 | tf_op jit(solution)/shard_map/ppermute | solution.py:49
where the time goes:
time: 474 us; the launch traced here: 470 us
  waiting for transfers between devices  244 us (51%)
  local copies, waits for them, and re-layouts  113 us (24%)
  matrix products  57.3 us (12%)
  other arithmetic  45.7 us (10%)
  starting transfers between devices  9.6 us (2%)
    all_to_all x1, waiting for transfers between devices, device_step(): returned = lax.all_to_all(expert_out, 'ep', 2, 1, tiled=True)  200 us
    gather x4, local copies, waits for them, and re-layouts, gated_sum(): exp_rows[id_blk, pos_blk]  71.5 us
    ppermute x1, waiting for transfers between devices, device_step(): arrived = lax.ppermute(combined, 'pp', send_next)  44.6 us
    reduce_sum x1, other arithmetic, gated_sum(): jnp.sum(weight[..., None] * picked.astype(jnp.float32), axis=3)  32.5 us
    all_to_all x1, local copies, waits for them, and re-layouts, device_step(): returned = lax.all_to_all(expert_out, 'ep', 2, 1, tiled=True)  20.5 us
    unnamed x11, local copies, waits for them, and re-layouts  20.5 us
    dot_general x1, matrix products, attention_block(): jnp.einsum('crif,ife->cre', attn_out, w_out, preferred_element_type=jnp.f...  17 us
    dot_general x1, matrix products, attention_block(): jnp.einsum('bqhe,bkhe->bhqk', q_heads, k_heads, preferred_element_type=jn...  15.5 us
  transfers between devices with their start and end apart: 2, of which 2 were waited for; matrix products, arithmetic and copies ran while one was open for 0% of the time, Pallas kernels for 0%

commit v1 on v0

v1 whole, which is shorter than its diff:
```python
import functools

import jax
import jax.numpy as jnp
from jax import lax
from jax.experimental import pallas as pl
from jax.experimental.pallas import tpu as pltpu
from jax.sharding import PartitionSpec as P

NORM_EPS = 1e-6
MESH = pl.DeviceIdType.MESH
BF16 = jnp.bfloat16
F32 = jnp.float32


PARTS = (4, 4)
SCHEDULE = (2, 2, (1, 1))


def fused_kernel(stages, o_ref, idx_ref, slot_ref, gate_ref, h_ref, nw_ref, wq_ref, wk_ref, wv_ref, wo_ref, z_ref,
                 obx, obo, rtab_i, rtab_s, rtab_g, gate_tab, tot, xb, qb, kb, vb, wb,
                 snd0, snd1, rcv0, rcv1, own1, hbuf0, hbuf1, yb0, yb1, ab0, ab1, zbuf,
                 tab_s, tab_r, h_sem, loc_x, loc_o, dx_s, dx_r, do_s, do_r, x_s, x_r, y_s, y_r, r_s, r_r,
                 a_s, a_r, z_l, z_s, z_r, w_sem):
    snd, rcv, own, hbuf = (snd0, snd1), (rcv0, rcv1), (None, own1), (hbuf0, hbuf1)
    yb, ab, zb = (yb0, yb1), (ab0, ab1), (zbuf, zbuf)
    n_chunk, _, src, width = obx.shape
    n_exp, cap, d_model = o_ref.shape
    n_rows = 2 * n_exp * src
    tokens = h_ref.shape[0]
    size = [tokens * p // sum(PARTS) for p in PARTS]
    base = [sum(size[:p]) for p in range(2)]
    n_pick = idx_ref.shape[0]
    n_pair = kb.shape[1]
    head_dim = wq_ref.shape[2]
    scale = head_dim ** -0.5
    stage = lax.axis_index('pp')
    me = lax.axis_index('ep')
    chip = me // 2
    core = me % 2
    sib = chip * 2 + (1 - core)
    peer = (1 - chip) * 2 + core
    sib_peer = (1 - chip) * 2 + (1 - core)
    to_sib = {'pp': stage, 'ep': sib}
    to_peer = {'pp': stage, 'ep': peer}
    to_next = {'pp': (stage + 1) % stages, 'ep': me}
    to_prev = {'pp': (stage + stages - 1) % stages, 'ep': me}

    def remote(a, b, send, recv, dev):
        return pltpu.make_async_remote_copy(a, b, send, recv, device_id=dev, device_id_type=MESH)

    def rows_of(owner, k):
        return o_ref.at[:, pl.ds(pl.multiple_of(owner * src, 8), src), pl.ds(pl.multiple_of(k * width, width), width)]

    def half_of(buf, k, core_idx):
        return buf.at[k, pl.ds(core_idx * n_exp, n_exp)]

    def load_pair(i, s):
        for m, w in enumerate((wq_ref, wk_ref, wv_ref)):
            for t in range(2):
                pltpu.make_async_copy(
                    w.at[core * (2 * n_pair) + 2 * i + t],
                    wb.at[s, :, pl.ds(m * width + t * head_dim, head_dim)], w_sem.at[s, m]).start()

    def tile_slot(p, n):
        return (p + 1 + n // 3) % 3, n % 3

    def load_tile(p, n):
        s, m = tile_slot(p, n)
        pltpu.make_async_copy(
            wo_ref.at[:, pl.ds(pl.multiple_of((core * n_pair + n) * width, width), width)],
            wb.at[s, :, pl.ds(m * width, width)], w_sem.at[s, m]).start()

    def wait_tile(s, m):
        dst = wb.at[s, :, pl.ds(m * width, width)]
        pltpu.make_async_copy(dst, dst, w_sem.at[s, m]).wait()

    def build(idx, slot, gate, owner, out, parts):
        first = chip * (2 * n_exp)
        keep = (slot >= 0) & (idx >= first) & (idx < first + 2 * n_exp)
        key = jnp.where(keep, (idx - first) * src + (slot - owner * src), -1)
        key_t = key.T
        gate_t = gate.T
        rows = 64
        for p in parts:
            for low in range(0, size[p], rows):
                kr = key_t[base[p] + low:base[p] + low + rows]
                gr = gate_t[base[p] + low:base[p] + low + rows]
                for b in range(n_rows // 128):
                    lane = lax.broadcasted_iota(jnp.int32, (rows, 128), 1) + b * 128
                    acc = jnp.zeros((rows, 128), F32)
                    for i in range(n_pick):
                        acc = jnp.where(kr[:, i:i + 1] == lane, gr[:, i:i + 1], acc)
                    for t in range(3):
                        top = acc.astype(BF16)
                        at = 3 * base[p] + t * size[p] + low
                        out[at:at + rows, b * 128:(b + 1) * 128] = top
                        acc = acc - top.astype(F32)

    def mix(table, buf, k, parts):
        low, high = 3 * base[parts[0]], 3 * (base[parts[-1]] + size[parts[-1]])
        full = jnp.dot(table[low:high], buf[k].reshape(n_rows, width), preferred_element_type=F32)
        out = []
        for p in parts:
            n, at = size[p], 3 * base[p] - low
            out.append((full[at + 2 * n:at + 3 * n] + full[at + n:at + 2 * n]) + full[at:at + n])
        return out

    def wait_rows(buf, loc, send, recv, k):
        mine = half_of(buf, k, core)
        pltpu.make_async_copy(mine, mine, loc.at[k]).wait()
        other = half_of(buf, k, 1 - core)
        remote(other, other, send.at[k], recv.at[k], to_sib).wait_recv()

    def send_part(p, k):
        g = p * n_chunk + k
        return remote(snd[p].at[k], rcv[p].at[k], x_s.at[g], x_r.at[g], to_peer)

    def y_slot(p, k, whose):
        return yb[p].at[k, pl.ds(pl.multiple_of(whose * size[p], size[p]), size[p])]

    def send_y(p, k):
        g = p * n_chunk + k
        return remote(hbuf[p].at[k], y_slot(p, k, core), y_s.at[g], y_r.at[g], to_next)

    def relay_copy(p, k):
        g = p * n_chunk + k
        return remote(y_slot(p, k, core), y_slot(p, k, core), r_s.at[g], r_r.at[g], to_sib)

    def chunk(p, k):
        if p == 0:
            wait_rows(obo, loc_o, do_s, do_r, k)
            mine, own[1][k] = mix(gate_tab, obo, k, (0, 1))
        else:
            mine = own[p][k]
        send_part(p, k).wait_recv()
        hbuf[p][k] = (hbuf[p][k].astype(F32) + (mine + rcv[p][k])).astype(BF16)
        send_y(p, k).start()

    def relay(p, k):
        send_y(p, k).wait_recv()
        relay_copy(p, k).start()

    def squares(p, k0, k1):
        @pl.loop(k0, k1)
        def _(k):
            g = p * n_chunk + k
            other = y_slot(p, k, 1 - core)
            remote(other, other, r_s.at[g], r_r.at[g], to_sib).wait_recv()
        n = 2 * size[p]
        total = jnp.zeros((n, width), F32) if k0 == 0 else tot[:n]
        for k in range(k0, k1):
            y = yb[p][k].astype(F32)
            total = total + y * y
        tot[:n] = total

    def normed(p):
        n = 2 * size[p]
        inv = lax.rsqrt(jnp.sum(tot[:n], axis=-1, keepdims=True) * (1.0 / d_model) + NORM_EPS)
        for k in range(n_chunk):
            y = yb[p][k].astype(F32)
            cols = slice(k * width, (k + 1) * width)
            xb[:n, cols] = (y * inv * nw_ref[:, cols]).astype(BF16)

    def send_heads(p, i):
        cols = pl.ds(pl.multiple_of((core * n_pair + i) * width, width), width)
        j = p * n_pair + i
        return remote(ab[p].at[:, cols], ab[p].at[:, cols], a_s.at[j], a_r.at[j], to_sib)

    def wait_heads(p):
        for i in range(n_pair):
            cols = pl.ds(pl.multiple_of(((1 - core) * n_pair + i) * width, width), width)
            dst = ab[p].at[:, cols]
            j = p * n_pair + i
            remote(dst, dst, a_s.at[j], a_r.at[j], to_sib).wait_recv()

    def wait_set(s):
        for m in range(3):
            wait_tile(s, m)

    def attend(p, i):
        n, low = size[p], base[p]
        keys = tokens
        row = lax.broadcasted_iota(jnp.int32, (n, keys), 0) + low
        col = lax.broadcasted_iota(jnp.int32, (n, keys), 1)
        for q in range(2):
            for t in range(2):
                hd = slice(t * head_dim, (t + 1) * head_dim)
                qh = qb[q * n:(q + 1) * n, hd]
                kh = kb[q, i, :keys, hd]
                vh = vb[q, i, :keys, hd]
                sc = lax.dot_general(qh, kh, (((1,), (1,)), ((), ())), preferred_element_type=F32) * scale
                sc = jnp.where(row >= col, sc, -jnp.inf)
                e = jnp.exp(sc - jnp.max(sc, axis=-1, keepdims=True))
                e = (e * (1.0 / jnp.sum(e, axis=-1, keepdims=True))).astype(BF16)
                out = jnp.dot(e, vh, preferred_element_type=F32).astype(BF16)
                ab[p][q * n:(q + 1) * n,
                      pl.ds(pl.multiple_of((core * n_pair + i) * width + t * head_dim, head_dim), head_dim)] = out

    def heads(p, i):
        s = (i + p) % 3
        n, low = size[p], base[p]
        x = xb[:2 * n]
        out = [jnp.dot(x, wb[s, :, m * width:(m + 1) * width], preferred_element_type=F32).astype(BF16) for m in range(3)]
        qb[:2 * n] = out[0]
        for q in range(2):
            kb[q, i, low:low + n, :] = out[1][q * n:(q + 1) * n]
            vb[q, i, low:low + n, :] = out[2][q * n:(q + 1) * n]

    def pair(p, i):
        wait_set((i + p) % 3)
        attend(p, i - 1)
        heads(p, i)
        send_heads(p, i - 1).start()

        @pl.when(i < n_pair - 3)
        def _():
            load_pair(i + 3, (i + p) % 3)

        @pl.when(i == n_pair - 3)
        def _():
            for n in range(3):
                load_tile(p, n)

        @pl.when(i == n_pair - 2)
        def _():
            for n in range(3, 6):
                load_tile(p, n)

        @pl.when(i == n_pair - 1)
        def _():
            load_tile(p, 6)

    def first_pair(p):
        wait_set(p)
        heads(p, 0)
        load_pair(3, p)

    def last_pair(p):
        attend(p, n_pair - 1)
        send_heads(p, n_pair - 1).start()

    def z_copies(p, n):
        cols = pl.ds(pl.multiple_of((core * n_pair + n) * width, width), width)
        dst = z_ref.at[pl.ds(base[p], size[p]), cols]
        j = p * n_pair + n
        keep = zb[p].at[n, pl.ds(pl.multiple_of(core * size[p], size[p]), size[p])]
        give = zb[p].at[n, pl.ds(pl.multiple_of((1 - core) * size[p], size[p]), size[p])]
        return pltpu.make_async_copy(keep, dst, z_l.at[j]), remote(give, dst, z_s.at[j], z_r.at[j], to_sib)

    def half_dot(p, n, whose):
        s, m = tile_slot(p, n)
        cut = pl.ds(pl.multiple_of(whose * (d_model // 2), width), d_model // 2)
        return jnp.dot(ab[p][:, cut], wb[s, cut, m * width:(m + 1) * width], preferred_element_type=F32)

    def project_own(p, tiles):
        for n in tiles:
            wait_tile(*tile_slot(p, n))
        for n in tiles:
            own[1][2 * n], own[1][2 * n + 1] = jnp.split(half_dot(p, n, core), 2)

    def project(p, tiles, early):
        if not early:
            for n in tiles:
                wait_tile(*tile_slot(p, n))
        for n in tiles:
            s, m = tile_slot(p, n)
            if early:
                out = (jnp.concatenate((own[1][2 * n], own[1][2 * n + 1])) + half_dot(p, n, 1 - core)).astype(BF16)
            else:
                out = jnp.dot(ab[p][...], wb[s, :, m * width:(m + 1) * width], preferred_element_type=F32).astype(BF16)
            y = yb[p][core * n_pair + n].astype(F32)
            zb[p][n] = (y + out.astype(F32)).astype(BF16)
        for n in tiles:
            for c in z_copies(p, n):
                c.start()
            if p == 0 and n % 3 == 2:
                load_pair(n // 3, (n // 3 + 1) % 3)
            if p == 0 and n == 6:
                load_pair(2, 0)

    def drain_z(p):
        for n in range(n_pair):
            send_heads(p, n).wait_send()
            keep, give = z_copies(p, n)
            keep.wait()
            give.wait()

    barrier = pltpu.get_barrier_semaphore()
    for dev in (to_sib, to_peer, to_next, to_prev):
        pl.semaphore_signal(barrier, inc=1, device_id=dev, device_id_type=MESH)

    @pl.loop(0, n_chunk)
    def _(k):
        pltpu.make_async_copy(rows_of(peer, k), half_of(obx, k, core), loc_x.at[k]).start()

    pl.semaphore_wait(barrier, 4)

    tabs = [remote(a, b, tab_s.at[i], tab_r.at[i], to_peer)
            for i, (a, b) in enumerate(((idx_ref, rtab_i), (slot_ref, rtab_s), (gate_ref, rtab_g)))]
    for t in tabs:
        t.start()

    @pl.loop(0, n_chunk)
    def _(k):
        remote(rows_of(sib_peer, k), half_of(obx, k, core), dx_s.at[k], dx_r.at[k], to_sib).start()

    for p in range(2):
        @pl.loop(0, n_chunk)
        def _(k):
            pltpu.make_async_copy(
                h_ref.at[pl.ds(base[p], size[p]), pl.ds(pl.multiple_of(k * width, width), width)],
                hbuf[p].at[k], h_sem.at[p]).start()

    @pl.loop(0, n_chunk)
    def _(k):
        pltpu.make_async_copy(rows_of(me, k), half_of(obo, k, core), loc_o.at[k]).start()
        remote(rows_of(sib, k), half_of(obo, k, core), do_s.at[k], do_r.at[k], to_sib).start()

    for t in tabs:
        t.wait()
    build(rtab_i[...], rtab_s[...], rtab_g[...], peer, gate_tab, (0,))
    ahead = 2

    @pl.loop(0, ahead)
    def _(k):
        wait_rows(obx, loc_x, dx_s, dx_r, k)
        snd[0][k], = mix(gate_tab, obx, k, (0,))
        send_part(0, k).start()

    build(rtab_i[...], rtab_s[...], rtab_g[...], peer, gate_tab, (1,))

    @pl.loop(ahead, n_chunk)
    def _(k):
        wait_rows(obx, loc_x, dx_s, dx_r, k)
        snd[0][k], snd[1][k] = mix(gate_tab, obx, k, (0, 1))
        send_part(0, k).start()

    @pl.loop(0, ahead)
    def _(k):
        snd[1][k], = mix(gate_tab, obx, k, (1,))

    for i in range(3):
        load_pair(i, i)
    build(idx_ref[...], slot_ref[...], gate_ref[...], me, gate_tab, (0, 1))
    for p in range(2):
        pltpu.make_async_copy(hbuf[p], hbuf[p], h_sem.at[p]).wait()

    for q in range(2):
        @pl.loop(0, n_pair)
        def _(i):
            kb[q, i, base[1]:, :] = jnp.zeros((size[1], width), BF16)
            vb[q, i, base[1]:, :] = jnp.zeros((size[1], width), BF16)

    @pl.loop(0, n_chunk)
    def _(k):
        send_part(1, k).start()
        chunk(0, k)

        @pl.when(k >= 2)
        def _():
            relay(0, k - 2)

    lead, lag, counts = SCHEDULE

    def step(k):
        chunk(1, k)
        if isinstance(k, int):
            if k >= lag:
                relay(1, k - lag)
        else:
            @pl.when(k >= lag)
            def _():
                relay(1, k - lag)

    for k in range(lead):
        step(k)
        if k >= lead - 2:
            relay(0, n_chunk - lead + k)

    squares(0, 0, n_chunk)
    normed(0)
    first_pair(0)
    each = counts[0] + counts[1]

    @pl.loop(0, 3)
    def _(j):
        for h in range(2):
            for c in range(counts[h]):
                step(lead + each * j + h * counts[0] + c)
            pair(0, 2 * j + 1 + h)

    k = lead + 3 * each
    rest = [lambda: last_pair(0), lambda: wait_heads(0), lambda: project(0, (0, 1, 2), False),
            lambda: project(0, (3, 4, 5), False), lambda: project(0, (6,), False)]
    done = k - lag
    for job in rest:
        if k < n_chunk:
            step(k)
            done = k - lag + 1
            k += 1
        elif done < n_chunk - 2:
            relay(1, done)
            done += 1
        job()
    while k < n_chunk:
        step(k)
        done = k - lag + 1
        k += 1

    @pl.loop(0, n_chunk)
    def _(k):
        for buf, s, r in ((obx, dx_s, dx_r), (obo, do_s, do_r)):
            mine = half_of(buf, k, core)
            remote(mine, mine, s.at[k], r.at[k], to_sib).wait_send()
        for p in range(2):
            send_part(p, k).wait_send()
        send_y(0, k).wait_send()
        relay_copy(0, k).wait_send()

    while done < n_chunk - 2:
        relay(1, done)
        done += 1
    squares(1, 0, n_chunk - 2)
    relay(1, n_chunk - 2)
    relay(1, n_chunk - 1)
    squares(1, n_chunk - 2, n_chunk)
    normed(1)
    first_pair(1)

    @pl.loop(1, n_pair)
    def _(i):
        pair(1, i)

    last_pair(1)
    drain_z(0)
    project_own(1, (0, 1, 2))

    @pl.loop(0, n_chunk)
    def _(k):
        send_y(1, k).wait_send()
        relay_copy(1, k).wait_send()

    wait_heads(1)
    project(1, (0, 1, 2), True)
    project(1, (3, 4, 5), False)
    project(1, (6,), False)
    drain_z(1)


def fused_block(stages, expert_out, expert_ids, slot_ids, gate_vals, residual, norm_w, w_query, w_key, w_value, w_out):
    n_exp, cap, d_model = expert_out.shape
    tokens = residual.shape[0]
    n_head, _, head_dim = w_query.shape
    width = 2 * head_dim
    n_chunk = d_model // width
    n_pair = n_head // 4
    size = [tokens * p // sum(PARTS) for p in PARTS]
    n_rows = 2 * n_exp * (cap // 4)
    n_pick = expert_ids.shape[0]
    dma = pltpu.SemaphoreType.DMA
    any_spec = pl.BlockSpec(memory_space=pl.ANY)
    vmem_spec = pl.BlockSpec(memory_space=pltpu.VMEM)
    vm = pltpu.VMEM

    def per_part(make):
        return [make(n) for n in size]

    return pl.pallas_call(
        functools.partial(fused_kernel, stages),
        out_shape=jax.ShapeDtypeStruct((tokens, d_model), BF16),
        in_specs=[any_spec, vmem_spec, vmem_spec, vmem_spec, any_spec, vmem_spec] + [any_spec] * 4,
        out_specs=any_spec,
        scratch_shapes=[
            vm((n_chunk, 2 * n_exp, cap // 4, width), BF16),
            vm((n_chunk, 2 * n_exp, cap // 4, width), BF16),
            vm((n_pick, tokens), jnp.int32),
            vm((n_pick, tokens), jnp.int32),
            vm((n_pick, tokens), F32),
            vm((3 * tokens, n_rows), BF16),
            vm((tokens, width), F32),
            vm((tokens, d_model), BF16),
            vm((tokens, width), BF16),
            vm((2, n_pair, tokens, width), BF16),
            vm((2, n_pair, tokens, width), BF16),
            vm((3, d_model, 3 * width), BF16),
        ] + per_part(lambda n: vm((n_chunk, n, width), F32)) * 2
          + per_part(lambda n: vm((n_chunk, n, width), F32))[1:]
          + per_part(lambda n: vm((n_chunk, n, width), BF16))
          + per_part(lambda n: vm((n_chunk, 2 * n, width), BF16))
          + per_part(lambda n: vm((2 * n, d_model), BF16))
          + [vm((n_pair, 2 * max(size), width), BF16)]
          + [dma((3,)), dma((3,)), dma((2,))]
          + [dma((n_chunk,))] * 6 + [dma((2 * n_chunk,))] * 6 + [dma((2 * n_pair,))] * 5 + [dma((3, 3))],
        compiler_params=pltpu.CompilerParams(collective_id=0, has_side_effects=True, vmem_limit_bytes=67_000_000),
        name='fused_block',
    )(expert_out, expert_ids, slot_ids, gate_vals, residual, norm_w, w_query, w_key, w_value, w_out)


def solution(mesh):
    stages = mesh.shape['pp']
    tok_spec = P('pp', 'ep', None, None)
    wt_spec = P('pp', None, None, None)

    def device_step(expert_out, expert_ids, slot_ids, gate_vals, residual, norm_w, w_query, w_key, w_value, w_out):
        heads = [w[0].transpose(1, 0, 2) for w in (w_query, w_key, w_value)]
        proj = w_out[0].reshape(-1, w_out.shape[3])
        result = fused_block(stages, expert_out[0], expert_ids[0, 0].T, slot_ids[0, 0].T, gate_vals[0, 0].T,
                             residual[0, 0], norm_w, *heads, proj)
        return result.reshape(residual.shape)

    return jax.shard_map(device_step, mesh=mesh, in_specs=(tok_spec, tok_spec, tok_spec, tok_spec, tok_spec, P('pp', None), wt_spec, wt_spec, wt_spec, wt_spec), out_specs=tok_spec, check_vma=False)
```

time: 474 us -> 126 us (0.27)
  waiting for transfers between devices: 244 us -> 0 us
  Pallas kernels: 0 us -> 123 us
  local copies, waits for them, and re-layouts: 113 us -> 2.85 us
  matrix products: 57.3 us -> 0 us
  other arithmetic: 45.7 us -> 0 us
  starting transfers between devices: 9.6 us -> 0 us
    all_to_all x1 -> x0, waiting for transfers between devices: 200 us -> none  [device_step(): returned = lax.all_to_all(expert_out, 'ep', 2, 1, tiled=True)]
    pallas_call x0 -> x1, Pallas kernels: none -> 123 us  [fused_block(): pl.pallas_call(functools.partial(fused_kernel, stages), out_shape=jax.Sha...]
    gather x4 -> x0, local copies, waits for them, and re-layouts: 71.5 us -> none  [gated_sum(): exp_rows[id_blk, pos_blk]]
    dot_general x4 -> x0, matrix products: 57.3 us -> none  [the longest x1 17 us: attention_block(): jnp.einsum('crif,ife->cre', attn_out, w_out, preferred_element_type=jnp.f...]
    ppermute x1 -> x0, waiting for transfers between devices: 44.6 us -> none  [device_step(): arrived = lax.ppermute(combined, 'pp', send_next)]
    reduce_sum x2 -> x0, other arithmetic: 34.4 us -> none  [the longest x1 32.5 us: gated_sum(): jnp.sum(weight[..., None] * picked.astype(jnp.float32), axis=3)]
    all_to_all x1 -> x0, local copies, waits for them, and re-layouts: 20.5 us -> none  [device_step(): returned = lax.all_to_all(expert_out, 'ep', 2, 1, tiled=True)]
    unnamed x11 -> x1, local copies, waits for them, and re-layouts: 20.5 us -> 2.85 us
  transfers between devices with their start and end apart: 2 -> 0, of which waited for: 2 -> 0; matrix products, arithmetic and copies ran while one was open for 0% -> 0% of each run, Pallas kernels for 0% -> 0%
where the time goes in v1:
time: 126 us; the launch traced here: 125 us
  Pallas kernels  123 us (98%)
  local copies, waits for them, and re-layouts  2.85 us (2%)
    pallas_call x1, Pallas kernels, fused_block(): pl.pallas_call(functools.partial(fused_kernel, stages), out_shape=jax.Sha...  123 us
    unnamed x1, local copies, waits for them, and re-layouts  2.85 us

profile of v1, /device:TPU:0, one launch (start us, length us, event | category | flops | bytes accessed | tf_op | source)
XLA Modules:
  0.0 125.4 jit_solution(18298352398931184168)
XLA Ops:
  0.0 122.6 %fused_block.1 = bf16[256,3584]{1,0:T(8,128)(2,1)} custom-call(bf16[16,160,3584]{2,1,0:T(8,128)(2,1)} %bitcast.26, s32[8,256]{1,0:T(8,128)} %bitcast.29, s32[8,256]{1,0:T(8,128)} %bitcast.30, f32[8,256]{1,0:T(8,128)} %bitcast.31, bf16[256,3584]{1,0:T(8,128)(2,1)} %bitcast.28, f32[1,3584]{1,0:T(1,128)} %nw_ref.1, bf16[28,3584,128]{2,1,0:T(8,128)(2,1)} %bitcast.22, ...), custom_call_target="tpu_custom_call" | custom-call | tf_op jit(solution)/shard_map/fused_block/pallas_call | solution.py:469
  122.6 2.8 %copy.12 = bf16[1,1,256,3584]{3,2,1,0:T(8,128)(2,1)} copy(bf16[1,1,256,3584]{3,2,1,0:T(8,128)(2,1)} %bitcast.27) | data formatting | bytes 3670016
